TPU v7x, 32 devices: a whole 2x2x4 slice. The times are simulated.
32 devices in a mesh: rows: 8 (over z, y), rep: 4 (over x, core).
Axes of the slice: x: 2, y: 2, z: 4, core: 2. Of those that a mesh axis runs over, the one named last changes fastest.
Arguments:
- event_slots: int32 [32, 128], P(('rows', 'rep')), may hold values from 0 to 143, as said below
- fetch_rows: int32 [32, 16], P(('rows', 'rep')), may hold values from 0 to 255, as said below
- fetch_counts: int32 [32, 8], P(('rows', 'rep')), may hold values from 1 to 2, as said below
- hot_table: float32 [128, 512], replicated, may hold values from -6 to 6
- hot_accum: float32 [128], replicated, may hold values from 0.05 to 2
- cold_table: float32 [2048, 512], P('rows'), may hold values from -6 to 6
- cold_accum: float32 [2048], P('rows'), may hold values from 0.05 to 2
- ln_gain: float32 [512], replicated, may hold values from 0.1 to 1.9
- ln_bias: float32 [512], replicated, may hold values from -3 to 3
- w_in: bfloat16 [512, 2048], replicated, may hold values from -0.25 to 0.25
- w_out: bfloat16 [512, 512], replicated, may hold values from -0.25 to 0.25
- out_grad: bfloat16 [4096, 512], P(('rows', 'rep')), may hold values from -6 to 6
Outputs:
- new_hot_table: float32 [128, 512], replicated
- new_hot_accum: float32 [128], replicated
- new_cold_table: float32 [2048, 512], P('rows')
- new_cold_accum: float32 [2048], P('rows')
Inputs may be any that keep to these rules, and one draw needn't show every extreme that they name: `event_slots`: rows of the lookup buffer: the 128 hot rows, then 2 slots for each of the 8 owners; an event names slot k of owner j only if k is below that device's fetch_counts for j. `fetch_rows`: rows local to the owner's shard, distinct within one owner's 2 slots of one device; slots at or past the count are padding. `fetch_counts`: some owner is asked for 2 rows by every device.
All inputs are finite; a program needn't handle non-finite values.
Results may differ from a plain program's by a relative error of at most 0.0065.
Values sent between devices are 32-bit elements; how exact they have to be, the bound alone decides.
No kernel may reach another device: no remote copies, remote signals or barrier semaphores. Data moves between devices by JAX's collectives and lax.ppermute only.
A program may use at most 64 MiB of HBM per device.

v0:
```python
import jax
import jax.numpy as jnp
from jax import lax
from jax.sharding import PartitionSpec as P

HEAD = 128
STEP_RATE = 0.5


def hstu_layer(looked_up, ln_gain, ln_bias, w_in, w_out):
    seq_rows = looked_up.shape[0]
    inner = w_out.shape[0]
    n_heads = inner // HEAD
    row_mean = jnp.mean(looked_up, axis=1, keepdims=True)
    centered = looked_up - row_mean
    row_var = jnp.mean(centered * centered, axis=1, keepdims=True)
    normed = (centered * lax.rsqrt(row_var + 1e-05) * ln_gain + ln_bias).astype(jnp.bfloat16)
    projected = jax.nn.silu(jnp.dot(normed, w_in, preferred_element_type=jnp.float32)).astype(
        jnp.bfloat16
    )
    gates_u, values_v, queries, keys_k = jnp.split(projected, 4, axis=1)
    head_shape = (seq_rows, n_heads, HEAD)
    scores = jnp.einsum(
        "qhd,khd->hqk",
        queries.reshape(head_shape),
        keys_k.reshape(head_shape),
        preferred_element_type=jnp.float32,
    ) * HEAD ** (-0.5)
    causal = (
        lax.broadcasted_iota(jnp.int32, (seq_rows, seq_rows), 0)
        >= lax.broadcasted_iota(jnp.int32, (seq_rows, seq_rows), 1)
    ).astype(jnp.float32)
    attention = (jax.nn.silu(scores) * causal * (1.0 / seq_rows)).astype(jnp.bfloat16)
    mixed_val = jnp.einsum(
        "hqk,khd->qhd", attention, values_v.reshape(head_shape), preferred_element_type=jnp.float32
    ).reshape(seq_rows, inner)
    mixed_mean = jnp.mean(mixed_val, axis=1, keepdims=True)
    mixed_cent = mixed_val - mixed_mean
    mixed_var = jnp.mean(mixed_cent * mixed_cent, axis=1, keepdims=True)
    gated_val = (mixed_cent * lax.rsqrt(mixed_var + 1e-06) * gates_u.astype(jnp.float32)).astype(
        jnp.bfloat16
    )
    layer_out = looked_up + jnp.dot(gated_val, w_out, preferred_element_type=jnp.float32)
    return layer_out.astype(jnp.bfloat16)


def adagrad(table_rows, accum_rows, grad_rows):
    new_accum = accum_rows + jnp.mean(grad_rows * grad_rows, axis=1)
    return (table_rows - STEP_RATE * grad_rows * lax.rsqrt(new_accum)[:, None], new_accum)


def on_device(
    event_slots,
    fetch_rows,
    fetch_counts,
    hot_table,
    hot_accum,
    cold_table,
    cold_accum,
    ln_gain,
    ln_bias,
    w_in,
    w_out,
    out_grad,
):
    owner_count = lax.axis_size("rows")
    per_owner = fetch_rows.shape[1] // owner_count
    hot_rows, feature_width = hot_table.shape
    rows_shard = cold_table.shape[0]
    wanted_rows = fetch_rows.reshape(owner_count, per_owner)
    live_mask = (
        lax.broadcasted_iota(jnp.int32, (owner_count, per_owner), 1)
        < fetch_counts.reshape(owner_count, 1)
    ).astype(jnp.float32)[:, :, None]
    asked_rows = lax.all_to_all(wanted_rows, "rows", split_axis=0, concat_axis=0, tiled=True)
    found = cold_table[asked_rows]
    fetched = lax.all_to_all(found, "rows", split_axis=0, concat_axis=0, tiled=True)
    buffer = jnp.concatenate(
        [hot_table, (fetched * live_mask).reshape(owner_count * per_owner, feature_width)], axis=0
    )
    event_rows = event_slots.reshape(-1)
    looked_up = buffer[event_rows]

    def forward(lookup_rows):
        return hstu_layer(lookup_rows, ln_gain, ln_bias, w_in, w_out)

    _, backward = jax.vjp(forward, looked_up)
    (d_lookup,) = backward(out_grad)
    buffer_grad = jax.ops.segment_sum(
        d_lookup, event_rows, num_segments=hot_rows + owner_count * per_owner
    )
    returned = buffer_grad[hot_rows:].reshape(owner_count, per_owner, feature_width) * live_mask
    arrived = lax.all_to_all(returned, "rows", split_axis=0, concat_axis=0, tiled=True)
    cold_grad = jax.ops.segment_sum(
        arrived.reshape(-1, feature_width), asked_rows.reshape(-1), num_segments=rows_shard
    )
    hot_grad = buffer_grad[:hot_rows]
    group_sum = lax.psum(hot_grad, "rep")
    my_share = lax.psum_scatter(group_sum, "rows", scatter_dimension=0, tiled=True)
    span_rows = my_share.shape[0]
    first_row = lax.axis_index("rows") * span_rows
    own_rows = lax.dynamic_slice_in_dim(hot_table, first_row, span_rows, 0)
    own_accum = lax.dynamic_slice_in_dim(hot_accum, first_row, span_rows, 0)
    part_rows, part_accum = adagrad(own_rows, own_accum, my_share)
    new_hot_table, new_hot_accum = (
        lax.all_gather(part_rows, "rows", axis=0, tiled=True),
        lax.all_gather(part_accum, "rows", axis=0, tiled=True),
    )
    summed_cold = lax.psum(cold_grad, "rep")
    new_cold_table, new_cold_accum = adagrad(cold_table, cold_accum, summed_cold)
    return (new_hot_table, new_hot_accum, new_cold_table, new_cold_accum)


def solution(mesh):
    return jax.shard_map(
        on_device,
        mesh=mesh,
        in_specs=(
            P(("rows", "rep"), None),
            P(("rows", "rep"), None),
            P(("rows", "rep"), None),
            P(),
            P(),
            P("rows", None),
            P("rows"),
            P(),
            P(),
            P(),
            P(),
            P(("rows", "rep"), None),
        ),
        out_specs=(P(), P(), P("rows", None), P("rows")),
        check_vma=False,
    )
```

profile of v0, /device:TPU:0, one launch (start us, length us, event | category | flops | bytes accessed | tf_op | source)
XLA Modules:
  0.0 198.6 jit_solution(12410957981415220685)
XLA Ops:
  8.0 0.5 broadcast.203
  8.5 1.4 reduce.10
  10.0 0.7 all_to_all.14
  10.6 7.3 %all-to-all-start = ((s32[8,1,2]{2,1,0:T(1,128)}), s32[8,1,2]{2,1,0:T(1,128)S(1)}, u32[]{:S(2)}, u32[]{:S(2)}) async-start(s32[8,1,2]{2,1,0:T(1,128)} %bitcast.1), calls=%async_computation | async-start | bytes 8192 | tf_op jit(solution)/shard_map/all_to_all | solution.py:75
  18.0 0.7 fusion.45
  18.6 0.7 fusion.44
  19.4 0.6 fusion.42
  20.0 4.4 %all-to-all-done = s32[8,1,2]{2,1,0:T(1,128)S(1)} async-done(((s32[8,1,2]{2,1,0:T(1,128)}), s32[8,1,2]{2,1,0:T(1,128)S(1)}, u32[]{:S(2)}, u32[]{:S(2)}) %all-to-all-start) | async-done | bytes 96 | tf_op jit(solution)/shard_map/all_to_all | solution.py:75
  24.6 1.6 gather_fusion
  26.3 0.6 reshape.204
  26.9 3.3 %all-to-all-start.1 = ((f32[8,2,512]{2,1,0:T(2,128)}), f32[8,2,512]{2,1,0:T(2,128)S(1)}, u32[]{:S(2)}, u32[]{:S(2)}) async-start(f32[8,2,512]{2,1,0:T(2,128)} %reshape.204), calls=%async_computation.1 | async-start | bytes 65536 | tf_op jit(solution)/shard_map/all_to_all | solution.py:77
  30.3 6.6 %all-to-all-done.1 = f32[8,2,512]{2,1,0:T(2,128)S(1)} async-done(((f32[8,2,512]{2,1,0:T(2,128)}), f32[8,2,512]{2,1,0:T(2,128)S(1)}, u32[]{:S(2)}, u32[]{:S(2)}) %all-to-all-start.1) | async-done | bytes 32800 | tf_op jit(solution)/shard_map/all_to_all | solution.py:77
  37.0 1.0 pad_maximum_fusion
  38.0 0.8 gather_fusion.1
  38.8 0.2 multiply_reduce_fusion.3
  39.1 1.5 multiply_convert_fusion
  40.6 0.8 copy-done.2
  41.6 0.2 convolution_multiply_fusion
  41.9 0.3 fusion.53
  42.3 0.3 copy-done.4
  42.6 0.1 copy.60
  42.8 1.5 multiply_reduce_fusion.2
  44.3 1.7 fusion.52
  46.0 0.3 convolution_convert_fusion.3
  46.4 0.3 fusion.19
  46.6 0.2 fusion.54
  46.8 0.2 fusion.55
  47.4 2.2 %multiply_reduce_fusion.1 = (f32[128]{0:T(128)S(1)}, f32[128,512]{1,0:T(8,128)S(1)}) fusion(f32[128,512]{1,0:T(8,128)S(1)} %gather_fusion.1, f32[128]{0:T(128)S(1)} %broadcast_multiply_fusion.3, f32[512]{0:T(512)S(1)} %copy-done.12, bf16[512,2048]{1,0:T(8,128)(2,1)S(1)} %copy-done, f32[128,2048]{1,0:T(8,128)} %get-tuple-element.19, ...), kind=kOutput, calls=%fused_computation.49 | convolution fusion | flops 273284992 | bytes 4197376 | tf_op jit(solution)/shard_map/transpose(jvp())/dot_general | solution.py:18
  49.7 0.2 fusion.51
  49.9 1.6 scatter_custom_fusion
  51.5 0.7 broadcast_multiply_fusion
  52.2 3.5 %all-to-all-start.2 = ((f32[8,2,512]{2,1,0:T(2,128)}), f32[8,2,512]{2,1,0:T(2,128)S(1)}, u32[]{:S(2)}, u32[]{:S(2)}) async-start(f32[8,2,512]{2,1,0:T(2,128)} %broadcast_multiply_fusion), calls=%async_computation.2 | async-start | bytes 65536 | tf_op jit(solution)/shard_map/all_to_all | solution.py:93
  55.8 0.7 reduce.11
  56.5 5.8 %all-to-all-done.2 = f32[8,2,512]{2,1,0:T(2,128)S(1)} async-done(((f32[8,2,512]{2,1,0:T(2,128)}), f32[8,2,512]{2,1,0:T(2,128)S(1)}, u32[]{:S(2)}, u32[]{:S(2)}) %all-to-all-start.2) | async-done | bytes 32800 | tf_op jit(solution)/shard_map/all_to_all | solution.py:93
  62.4 1.5 scatter_custom_fusion.1
  63.9 0.6 dynamic-slice
  65.2 0.7 slice.12
  65.9 28.9 %all-reduce.3.cloned.1.call-done = f32[256,512]{1,0:T(8,128)} async-done(((f32[256,512]{1,0:T(8,128)}), f32[256,512]{1,0:T(8,128)}) %all-reduce.3.cloned.1.call-update) | async-done | bytes 524304 | tf_op jit(solution)/shard_map/psum | solution.py:109
  94.8 1.2 multiply_reduce_fusion
  95.9 0.6 rsqrt_multiply_fusion
  96.5 1.9 multiply_subtract_fusion
  98.5 29.3 %reduce-scatter.2.cloned.1.call-done = f32[16,512]{1,0:T(8,128)} async-done(((f32[128,512]{1,0:T(8,128)}), f32[16,512]{1,0:T(8,128)}) %reduce-scatter.2.cloned.1.call-update) | async-done | bytes 32784 | tf_op jit(solution)/shard_map/reduce_scatter | solution.py:99
  127.7 10.8 %psum.16 = f32[16,512]{1,0:T(8,128)S(1)} all-reduce(f32[16,512]{1,0:T(8,128)} %reduce-scatter.2.cloned.1.call-done), channel_id=1, replica_groups=mesh['rows'=8,'rep'=4] {'rep'}, use_global_device_ids=true, to_apply=%region_9.10 | all-reduce | flops 8192 | bytes 65536 | tf_op jit(solution)/shard_map/psum | solution.py:98
  138.7 0.2 fusion.50
  138.8 0.8 multiply_subtract_fusion.1
  139.7 19.9 %all-reduce = f32[128]{0:T(128)} all-reduce(f32[128]{0:T(128)S(1)} %get-tuple-element.14), channel_id=1, replica_groups=mesh['rows'=8,'rep'=4] {'rows'}, use_global_device_ids=true, to_apply=%add | all-reduce | flops 128 | bytes 1024
  159.6 30.8 %all_gather.6 = f32[128,512]{1,0:T(8,128)S(1)} all-gather(f32[16,512]{1,0:T(8,128)S(1)} %multiply_subtract_fusion.1), channel_id=1, replica_groups=mesh['rows'=8,'rep'=4] {'rows'}, dimensions={0}, use_global_device_ids=true | all-gather | bytes 294912 | tf_op jit(solution)/shard_map/all_gather | solution.py:106
  190.4 0.7 copy.91
  (60 shorter events, 1.7 us)
Async XLA Ops:
  8.0 31.0 %copy-start = (bf16[512,2048]{1,0:T(8,128)(2,1)S(1)}, bf16[512,2048]{1,0:T(8,128)(2,1)}, u32[]{:S(2)}) copy-start(bf16[512,2048]{1,0:T(8,128)(2,1)} %param.21) | copy-start | bytes 6291460
  10.6 13.7 %all-to-all-start = ((s32[8,1,2]{2,1,0:T(1,128)}), s32[8,1,2]{2,1,0:T(1,128)S(1)}, u32[]{:S(2)}, u32[]{:S(2)}) async-start(s32[8,1,2]{2,1,0:T(1,128)} %bitcast.1), calls=%async_computation | async-start | bytes 8192 | tf_op jit(solution)/shard_map/all_to_all | solution.py:75
  17.9 21.1 %copy-start.11 = (f32[512]{0:T(512)S(1)}, f32[512]{0:T(512)}, u32[]{:S(2)}) copy-start(f32[512]{0:T(512)} %param.20) | copy-start | bytes 6148
  17.9 21.1 %copy-start.12 = (f32[512]{0:T(512)S(1)}, f32[512]{0:T(512)}, u32[]{:S(2)}) copy-start(f32[512]{0:T(512)} %param.19) | copy-start | bytes 6148
  26.9 10.0 %all-to-all-start.1 = ((f32[8,2,512]{2,1,0:T(2,128)}), f32[8,2,512]{2,1,0:T(2,128)S(1)}, u32[]{:S(2)}, u32[]{:S(2)}) async-start(f32[8,2,512]{2,1,0:T(2,128)} %reshape.204), calls=%async_computation.1 | async-start | bytes 65536 | tf_op jit(solution)/shard_map/all_to_all | solution.py:77
  40.6 0.8 copy-start.2
  40.6 2.1 %copy-start.3 = (bf16[128,512]{1,0:T(8,128)(2,1)S(1)}, bf16[128,512]{1,0:T(8,128)(2,1)}, u32[]{:S(2)}) copy-start(bf16[128,512]{1,0:T(8,128)(2,1)} %param.23) | copy-start | bytes 393220
  41.4 2.9 %copy-start.6 = (bf16[16,4,8,128]{3,2,1,0:T(8,128)(2,1)}, bf16[16,4,8,128]{3,2,1,0:T(8,128)(2,1)S(1)}, u32[]{:S(2)}) copy-start(bf16[16,4,8,128]{3,2,1,0:T(8,128)(2,1)S(1)} %get-tuple-element.11) | copy-start | bytes 393220
  41.9 0.7 copy-start.4
  42.7 3.3 %copy-start.5 = (f32[4,128,128]{2,1,0:T(8,128)S(1)}, f32[4,128,128]{2,1,0:T(8,128)}, u32[]{:S(2)}) copy-start(f32[4,128,128]{2,1,0:T(8,128)} %copy-done.4) | copy-start | bytes 786436
  42.7 3.6 %copy-start.8 = (f32[128,128]{1,0:T(8,128)S(1)}, f32[128,128]{1,0:T(8,128)}, u32[]{:S(2)}) copy-start(f32[128,128]{1,0:T(8,128)} %fusion.42) | copy-start | bytes 196612
  44.3 2.1 %copy-start.7 = (bf16[16,4,8,128]{3,2,1,0:T(8,128)(2,1)S(1)}, bf16[16,4,8,128]{3,2,1,0:T(8,128)(2,1)}, u32[]{:S(2)}) copy-start(bf16[16,4,8,128]{3,2,1,0:T(8,128)(2,1)} %copy-done.6) | copy-start | bytes 393220
  49.6 14.3 %copy-start.13 = (u32[32]{0:T(128)S(1)}, u32[32]{0:T(128)}, u32[]{:S(2)}) copy-start(u32[32]{0:T(128)} %constant.60) | copy-start | bytes 388
  49.6 46.3 %copy-start.9 = (f32[256]{0:T(256)S(1)}, f32[256]{0:T(256)}, u32[]{:S(2)}) copy-start(f32[256]{0:T(256)} %param.18) | copy-start | bytes 3076
  49.6 46.9 %copy-start.1 = (f32[256,512]{1,0:T(8,128)S(1)}, f32[256,512]{1,0:T(8,128)}, u32[]{:S(2)}) copy-start(f32[256,512]{1,0:T(8,128)} %param.17) | copy-start | bytes 1572868
  52.2 86.4 %copy-start.10 = (f32[128]{0:T(128)S(1)}, f32[128]{0:T(128)}, u32[]{:S(2)}) copy-start(f32[128]{0:T(128)} %param.16) | copy-start | bytes 1540
  52.2 10.1 %all-to-all-start.2 = ((f32[8,2,512]{2,1,0:T(2,128)}), f32[8,2,512]{2,1,0:T(2,128)S(1)}, u32[]{:S(2)}, u32[]{:S(2)}) async-start(f32[8,2,512]{2,1,0:T(2,128)} %broadcast_multiply_fusion), calls=%async_computation.2 | async-start | bytes 65536 | tf_op jit(solution)/shard_map/all_to_all | solution.py:93
  55.7 39.1 %all-reduce.3.cloned.1.call-start = ((), (), s32[]{:S(2)}) async-start(), calls=%async_computation.4 | async-start | bytes 1048576 | tf_op jit(solution)/shard_map/psum | solution.py:109
  63.9 63.9 %reduce-scatter.2.cloned.1.call-start = ((), (), s32[]{:S(2)}) async-start(), calls=%async_computation.5 | async-start | bytes 294912 | tf_op jit(solution)/shard_map/reduce_scatter | solution.py:99
Sparse Core Ops, SparseCore 0:
  64.0 30.7 all-reduce.2
Sparse Core Ops, SparseCore 1:
  68.2 59.4 reduce-scatter.1
where the time goes:
time: 199 us
  waiting for transfers between devices  75 us (38%)
  blocking collectives  61.5 us (31%)
  between operations  16.5 us (8%)
  other arithmetic  16.1 us (8%)
  starting transfers between devices  14.2 us (7%)
  local copies, waits for them, and re-layouts  8.5 us (4%)
  matrix products  6.7 us (3%)
    all_gather x1, blocking collectives, on_device(): lax.all_gather(part_rows, 'rows', axis=0, tiled=True)  30.8 us
    reduce_scatter x1, waiting for transfers between devices, on_device(): lax.psum_scatter(group_sum, 'rows', scatter_dimension=0, tiled=True)  29.3 us
    psum x1, waiting for transfers between devices, on_device(): summed_cold = lax.psum(cold_grad, 'rep')  28.9 us
    unnamed x1, blocking collectives  19.9 us
    psum x1, blocking collectives, on_device(): group_sum = lax.psum(hot_grad, 'rep')  10.8 us
    all_to_all x1, starting transfers between devices, on_device(): lax.all_to_all(wanted_rows, 'rows', split_axis=0, concat_axis=0, tiled=True)  7.31 us
    all_to_all x1, waiting for transfers between devices, on_device(): lax.all_to_all(found, 'rows', split_axis=0, concat_axis=0, tiled=True)  6.61 us
    all_to_all x1, waiting for transfers between devices, on_device(): lax.all_to_all(returned, 'rows', split_axis=0, concat_axis=0, tiled=True)  5.82 us
  transfers between devices with their start and end apart: 5, of which 5 were waited for; matrix products, arithmetic and copies ran while one was open for 4% of the time, Pallas kernels for 0%

commit v1 on v0

--- a/solution.py
+++ b/solution.py
@@ -106,7 +106,11 @@
         lax.all_gather(part_rows, "rows", axis=0, tiled=True),
         lax.all_gather(part_accum, "rows", axis=0, tiled=True),
     )
-    summed_cold = lax.psum(cold_grad, "rep")
+    summed_cold = cold_grad
+    for hop in (1, 2):
+        summed_cold = summed_cold + lax.ppermute(
+            summed_cold, "rep", [(dev, dev ^ hop) for dev in range(4)]
+        )
     new_cold_table, new_cold_accum = adagrad(cold_table, cold_accum, summed_cold)
     return (new_hot_table, new_hot_accum, new_cold_table, new_cold_accum)
 

time: 199 us -> 189 us (0.950)
  waiting for transfers between devices: 75 us -> 63.5 us
    psum x1 -> x0, waiting for transfers between devices: 28.9 us -> none  [on_device(): summed_cold = lax.psum(cold_grad, 'rep')]
    reduce_scatter x1, waiting for transfers between devices: 29.3 us -> 46.7 us  [on_device(): lax.psum_scatter(group_sum, 'rows', scatter_dimension=0, tiled=True)]
  transfers between devices with their start and end apart: 5 -> 6, of which waited for: 5 -> 4; matrix products, arithmetic and copies ran while one was open for 4% -> 3% of each run, Pallas kernels for 0% -> 0%
where the time goes in v1:
time: 189 us; the launch traced here: 188 us
  waiting for transfers between devices  63.5 us (34%)
  blocking collectives  61.6 us (33%)
  other arithmetic  17.2 us (9%)
  starting transfers between devices  15.9 us (8%)
  between operations  15.2 us (8%)
  local copies, waits for them, and re-layouts  8.19 us (4%)
  matrix products  6.73 us (4%)
    reduce_scatter x1, waiting for transfers between devices, on_device(): lax.psum_scatter(group_sum, 'rows', scatter_dimension=0, tiled=True)  46.7 us
    all_gather x1, blocking collectives, on_device(): lax.all_gather(part_rows, 'rows', axis=0, tiled=True)  30.8 us
    unnamed x1, blocking collectives  20 us
    psum x1, blocking collectives, on_device(): group_sum = lax.psum(hot_grad, 'rep')  10.8 us
    all_to_all x1, starting transfers between devices, on_device(): lax.all_to_all(wanted_rows, 'rows', split_axis=0, concat_axis=0, tiled=True)  7.31 us
    all_to_all x1, waiting for transfers between devices, on_device(): lax.all_to_all(found, 'rows', split_axis=0, concat_axis=0, tiled=True)  6.56 us
    all_to_all x1, waiting for transfers between devices, on_device(): lax.all_to_all(returned, 'rows', split_axis=0, concat_axis=0, tiled=True)  5.87 us
    all_to_all x1, waiting for transfers between devices, on_device(): lax.all_to_all(wanted_rows, 'rows', split_axis=0, concat_axis=0, tiled=True)  4.34 us
  transfers between devices with their start and end apart: 6, of which 4 were waited for; matrix products, arithmetic and copies ran while one was open for 3% of the time, Pallas kernels for 0%

profile of v1, /device:TPU:0, one launch (start us, length us, event | category | flops | bytes accessed | tf_op | source)
XLA Modules:
  0.0 188.3 jit_solution(3573820887132300627)
XLA Ops:
  7.2 0.5 broadcast.203
  7.7 1.4 reduce.10
  9.1 0.7 all_to_all.14
  9.8 7.3 %all-to-all-start = ((s32[8,1,2]{2,1,0:T(1,128)}), s32[8,1,2]{2,1,0:T(1,128)S(1)}, u32[]{:S(2)}, u32[]{:S(2)}) async-start(s32[8,1,2]{2,1,0:T(1,128)} %bitcast.1), calls=%async_computation | async-start | bytes 8192 | tf_op jit(solution)/shard_map/all_to_all | solution.py:75
  17.2 0.7 fusion.45
  17.8 0.7 fusion.44
  18.6 0.6 fusion.42
  19.2 4.3 %all-to-all-done = s32[8,1,2]{2,1,0:T(1,128)S(1)} async-done(((s32[8,1,2]{2,1,0:T(1,128)}), s32[8,1,2]{2,1,0:T(1,128)S(1)}, u32[]{:S(2)}, u32[]{:S(2)}) %all-to-all-start) | async-done | bytes 96 | tf_op jit(solution)/shard_map/all_to_all | solution.py:75
  23.8 1.6 gather_fusion
  25.4 0.6 reshape.204
  26.1 3.3 %all-to-all-start.1 = ((f32[8,2,512]{2,1,0:T(2,128)}), f32[8,2,512]{2,1,0:T(2,128)S(1)}, u32[]{:S(2)}, u32[]{:S(2)}) async-start(f32[8,2,512]{2,1,0:T(2,128)} %reshape.204), calls=%async_computation.1 | async-start | bytes 65536 | tf_op jit(solution)/shard_map/all_to_all | solution.py:77
  29.5 6.6 %all-to-all-done.1 = f32[8,2,512]{2,1,0:T(2,128)S(1)} async-done(((f32[8,2,512]{2,1,0:T(2,128)}), f32[8,2,512]{2,1,0:T(2,128)S(1)}, u32[]{:S(2)}, u32[]{:S(2)}) %all-to-all-start.1) | async-done | bytes 32800 | tf_op jit(solution)/shard_map/all_to_all | solution.py:77
  36.1 1.0 pad_maximum_fusion
  37.1 0.8 gather_fusion.1
  38.0 0.2 multiply_reduce_fusion.3
  38.3 1.5 multiply_convert_fusion
  39.8 0.7 copy-done.1
  40.8 0.2 convolution_multiply_fusion
  41.1 0.3 fusion.53
  41.4 0.6 fusion.21
  42.2 1.5 multiply_reduce_fusion.2
  43.7 0.7 fusion.47
  44.3 1.1 fusion.52
  45.5 0.3 convolution_convert_fusion.3
  45.8 0.3 fusion.19
  46.1 0.2 fusion.54
  46.3 0.2 fusion.55
  46.9 2.2 %multiply_reduce_fusion.1 = (f32[128]{0:T(128)S(1)}, f32[128,512]{1,0:T(8,128)S(1)}) fusion(f32[128,512]{1,0:T(8,128)S(1)} %gather_fusion.1, f32[128]{0:T(128)S(1)} %broadcast_multiply_fusion.3, f32[512]{0:T(512)S(1)} %copy-done.16, bf16[512,2048]{1,0:T(8,128)(2,1)S(1)} %copy-done, f32[128,2048]{1,0:T(8,128)} %get-tuple-element.21, ...), kind=kOutput, calls=%fused_computation.49 | convolution fusion | flops 273284992 | bytes 4197376 | tf_op jit(solution)/shard_map/transpose(jvp())/dot_general | solution.py:18
  49.2 0.2 fusion.51
  49.4 1.6 scatter_custom_fusion
  51.0 0.7 slice.12
  51.8 0.7 broadcast_multiply_fusion
  52.5 3.3 %all-to-all-start.2 = ((f32[8,2,512]{2,1,0:T(2,128)}), f32[8,2,512]{2,1,0:T(2,128)S(1)}, u32[]{:S(2)}, u32[]{:S(2)}) async-start(f32[8,2,512]{2,1,0:T(2,128)} %broadcast_multiply_fusion), calls=%async_computation.2 | async-start | bytes 65536 | tf_op jit(solution)/shard_map/all_to_all | solution.py:93
  55.8 0.7 reduce.11
  56.6 5.9 %all-to-all-done.2 = f32[8,2,512]{2,1,0:T(2,128)S(1)} async-done(((f32[8,2,512]{2,1,0:T(2,128)}), f32[8,2,512]{2,1,0:T(2,128)S(1)}, u32[]{:S(2)}, u32[]{:S(2)}) %all-to-all-start.2) | async-done | bytes 32800 | tf_op jit(solution)/shard_map/all_to_all | solution.py:93
  62.5 0.8 scatter_custom_fusion.1
  63.4 0.6 dynamic-slice
  64.7 46.7 %reduce-scatter.2.cloned.1.call-done = f32[16,512]{1,0:T(8,128)} async-done(((f32[128,512]{1,0:T(8,128)}), f32[16,512]{1,0:T(8,128)}) %reduce-scatter.2.cloned.1.call-update) | async-done | bytes 32784 | tf_op jit(solution)/shard_map/reduce_scatter | solution.py:99
  111.3 10.8 %psum.8 = f32[16,512]{1,0:T(8,128)S(1)} all-reduce(f32[16,512]{1,0:T(8,128)} %reduce-scatter.2.cloned.1.call-done), channel_id=1, replica_groups=mesh['rows'=8,'rep'=4] {'rep'}, use_global_device_ids=true, to_apply=%region_9.10 | all-reduce | flops 8192 | bytes 65536 | tf_op jit(solution)/shard_map/psum | solution.py:98
  122.3 1.1 add.102
  123.4 1.8 collective-permute-start.1
  125.3 0.8 multiply_subtract_fusion.1
  126.2 30.8 %all_gather.6 = f32[128,512]{1,0:T(8,128)S(1)} all-gather(f32[16,512]{1,0:T(8,128)S(1)} %multiply_subtract_fusion.1), channel_id=1, replica_groups=mesh['rows'=8,'rep'=4] {'rows'}, dimensions={0}, use_global_device_ids=true | all-gather | bytes 294912 | tf_op jit(solution)/shard_map/all_gather | solution.py:106
  156.9 20.0 %all-reduce = f32[128]{0:T(128)} all-reduce(f32[128]{0:T(128)S(1)} %get-tuple-element.16), channel_id=1, replica_groups=mesh['rows'=8,'rep'=4] {'rows'}, use_global_device_ids=true, to_apply=%add | all-reduce | flops 128 | bytes 1024
  177.0 1.2 multiply_reduce_fusion
  178.2 0.6 rsqrt_multiply_fusion
  178.8 1.9 %multiply_subtract_fusion = f32[256,512]{1,0:T(8,128)} fusion(f32[256,512]{1,0:T(8,128)} %param.17, f32[256,512]{1,0:T(8,128)S(1)} %get-tuple-element.7, f32[256]{0:T(256)S(1)} %get-tuple-element.4), kind=kLoop, calls=%fused_computation.30 | loop fusion | flops 262144 | bytes 1573888 | tf_op jit(solution)/shard_map/sub | solution.py:49
  180.7 0.7 copy.90
  (70 shorter events, 1.9 us)
Async XLA Ops:
  7.2 31.1 %copy-start = (bf16[512,2048]{1,0:T(8,128)(2,1)S(1)}, bf16[512,2048]{1,0:T(8,128)(2,1)}, u32[]{:S(2)}) copy-start(bf16[512,2048]{1,0:T(8,128)(2,1)} %param.21) | copy-start | bytes 6291460
  9.8 13.7 %all-to-all-start = ((s32[8,1,2]{2,1,0:T(1,128)}), s32[8,1,2]{2,1,0:T(1,128)S(1)}, u32[]{:S(2)}, u32[]{:S(2)}) async-start(s32[8,1,2]{2,1,0:T(1,128)} %bitcast.1), calls=%async_computation | async-start | bytes 8192 | tf_op jit(solution)/shard_map/all_to_all | solution.py:75
  17.1 21.1 %copy-start.14 = (f32[512]{0:T(512)S(1)}, f32[512]{0:T(512)}, u32[]{:S(2)}) copy-start(f32[512]{0:T(512)} %param.20) | copy-start | bytes 6148
  17.1 21.1 %copy-start.15 = (f32[512]{0:T(512)S(1)}, f32[512]{0:T(512)}, u32[]{:S(2)}) copy-start(f32[512]{0:T(512)} %param.19) | copy-start | bytes 6148
  17.1 23.9 %copy-start.5 = (f32[128,128]{1,0:T(8,128)}, f32[128,128]{1,0:T(8,128)S(1)}, u32[]{:S(2)}) copy-start(f32[128,128]{1,0:T(8,128)S(1)} %fusion.43) | copy-start | bytes 196612
  26.1 10.0 %all-to-all-start.1 = ((f32[8,2,512]{2,1,0:T(2,128)}), f32[8,2,512]{2,1,0:T(2,128)S(1)}, u32[]{:S(2)}, u32[]{:S(2)}) async-start(f32[8,2,512]{2,1,0:T(2,128)} %reshape.204), calls=%async_computation.1 | async-start | bytes 65536 | tf_op jit(solution)/shard_map/all_to_all | solution.py:77
  29.4 81.9 %reduce-scatter.2.cloned.1.call-start = ((), (), s32[]{:S(2)}) async-start(), calls=%async_computation.4 | async-start | bytes 294912 | tf_op jit(solution)/shard_map/reduce_scatter | solution.py:99
  38.2 1.6 copy-start.11
  38.2 1.5 copy-start.9
  39.8 0.8 copy-start.1
  39.8 2.3 %copy-start.2 = (bf16[128,512]{1,0:T(8,128)(2,1)S(1)}, bf16[128,512]{1,0:T(8,128)(2,1)}, u32[]{:S(2)}) copy-start(bf16[128,512]{1,0:T(8,128)(2,1)} %param.23) | copy-start | bytes 393220
  40.6 1.4 copy-start.3
  42.1 3.4 %copy-start.6 = (f32[128,128]{1,0:T(8,128)S(1)}, f32[128,128]{1,0:T(8,128)}, u32[]{:S(2)}) copy-start(f32[128,128]{1,0:T(8,128)} %copy-done.5) | copy-start | bytes 196612
  42.1 3.7 %copy-start.4 = (bf16[16,4,8,128]{3,2,1,0:T(8,128)(2,1)S(1)}, bf16[16,4,8,128]{3,2,1,0:T(8,128)(2,1)}, u32[]{:S(2)}) copy-start(bf16[16,4,8,128]{3,2,1,0:T(8,128)(2,1)} %copy-done.3) | copy-start | bytes 393220
  42.1 3.7 %copy-start.7 = (f32[128,128]{1,0:T(8,128)S(1)}, f32[128,128]{1,0:T(8,128)}, u32[]{:S(2)}) copy-start(f32[128,128]{1,0:T(8,128)} %fusion.42) | copy-start | bytes 196612
  45.8 1.1 copy-start.16
  46.9 2.2 %copy-start.12 = (f32[128]{0:T(128)S(1)}, f32[128]{0:T(128)}, u32[]{:S(2)}) copy-start(f32[128]{0:T(128)} %copy-done.11) | copy-start | bytes 1540
  46.9 2.3 %copy-start.10 = (f32[128]{0:T(128)S(1)}, f32[128]{0:T(128)}, u32[]{:S(2)}) copy-start(f32[128]{0:T(128)} %copy-done.9) | copy-start | bytes 1540
  49.1 14.3 %copy-start.17 = (u32[32]{0:T(128)S(1)}, u32[32]{0:T(128)}, u32[]{:S(2)}) copy-start(u32[32]{0:T(128)} %constant.60) | copy-start | bytes 388
  49.4 75.8 %copy-start.13 = (f32[128]{0:T(128)S(1)}, f32[128]{0:T(128)}, u32[]{:S(2)}) copy-start(f32[128]{0:T(128)} %param.16) | copy-start | bytes 1540
  52.5 10.0 %all-to-all-start.2 = ((f32[8,2,512]{2,1,0:T(2,128)}), f32[8,2,512]{2,1,0:T(2,128)S(1)}, u32[]{:S(2)}, u32[]{:S(2)}) async-start(f32[8,2,512]{2,1,0:T(2,128)} %broadcast_multiply_fusion), calls=%async_computation.2 | async-start | bytes 65536 | tf_op jit(solution)/shard_map/all_to_all | solution.py:93
  62.5 115.7 %copy-start.8 = (f32[256]{0:T(256)S(1)}, f32[256]{0:T(256)}, u32[]{:S(2)}) copy-start(f32[256]{0:T(256)} %param.18) | copy-start | bytes 3076
  63.3 58.9 %collective-permute-start = (f32[256,512]{1,0:T(8,128)S(1)}, f32[256,512]{1,0:T(8,128)}, u32[]{:S(2)}, u32[]{:S(2)}) collective-permute-start(f32[256,512]{1,0:T(8,128)S(1)} %scatter_custom_fusion.1), channel_id=1, source_target_pairs={{0,1},{1,0},{2,3},{3,2},{4,5},{5,4},{6,7},{7,6},{8,9},{9,8},{10,11... | collective-permute-start | bytes 1572872 | tf_op jit(solution)/shard_map/ppermute | solution.py:111
  123.4 53.6 %collective-permute-start.1 = (f32[256,512]{1,0:T(8,128)S(1)}, f32[256,512]{1,0:T(8,128)}, u32[]{:S(2)}, u32[]{:S(2)}) collective-permute-start(f32[256,512]{1,0:T(8,128)S(1)} %add.102), channel_id=1, source_target_pairs={{0,2},{1,3},{2,0},{3,1},{4,6},{5,7},{6,4},{7,5},{8,10},{9,11},{10,... | collective-permute-start | bytes 1572872 | tf_op jit(solution)/shard_map/ppermute | solution.py:111
Sparse Core Ops, SparseCore 0:
  51.9 59.3 reduce-scatter.1
